TPU v7x, 32 devices: a whole 2x2x4 slice. The times are simulated.
32 devices in a mesh: ep: 4 (over y, core), fsdp: 8 (over z, x).
Axes of the slice: x: 2, y: 2, z: 4, core: 2. Of those that a mesh axis runs over, the one named last changes fastest.
Arguments:
- master_down: float32 [16, 6400, 4096], P('ep', None, 'fsdp'), may hold values from -0.109375 to 0.109375
- second_down: bfloat16 [16, 6400, 4096], P('ep', None, 'fsdp'), may hold values from -0.0390625 to 0.0390625
- router_weight: float32 [4096, 16], P('fsdp', 'ep'), may hold values from -0.09375 to 0.09375
- router_gain: float32 [4096], P('fsdp'), may hold values from 0.25 to 1.75
Outputs:
- final_down: bfloat16 [16, 6400, 4096], P('ep', 'fsdp')
- scale_down: float32 [16, 6400], P('ep', 'fsdp')
- serve_router: bfloat16 [4096, 16], replicated
All inputs are finite; a program needn't handle non-finite values.
Results may differ from a plain program's by a relative error of at most 0.001.
Values may be sent and summed in bfloat16 or wider, within the bound.
No kernel may reach another device: no remote copies, remote signals or barrier semaphores. Data moves between devices by JAX's collectives and lax.ppermute only.
A program may use at most 256 MiB of HBM per device.

v0:
```python
import jax
import jax.numpy as jnp
from jax import lax
from jax.sharding import PartitionSpec as P


def shards(master_down, second_down, router_weight, router_gain):
    merged_down = master_down + second_down.astype(jnp.float32)
    total_down = lax.psum(jnp.sum(merged_down * merged_down, axis=2), "fsdp")
    scale_down = jnp.sqrt(total_down)
    narrow_down = (merged_down / jnp.expand_dims(scale_down, 2)).astype(jnp.bfloat16)
    final_down = lax.all_to_all(narrow_down, "fsdp", split_axis=1, concat_axis=2, tiled=True)
    scale_down = lax.dynamic_slice_in_dim(
        scale_down, lax.axis_index("fsdp") * final_down.shape[1], final_down.shape[1], axis=1
    )
    part_router = (router_weight * router_gain[:, None]).astype(jnp.bfloat16)
    row_router = lax.all_gather(part_router, "fsdp", axis=0, tiled=True)
    serve_router = lax.all_gather(row_router, "ep", axis=1, tiled=True)
    return (final_down, scale_down, serve_router)


def solution(mesh):
    return jax.shard_map(
        shards,
        mesh=mesh,
        in_specs=(P("ep", None, "fsdp"), P("ep", None, "fsdp"), P("fsdp", "ep"), P("fsdp")),
        out_specs=(P("ep", "fsdp", None), P("ep", "fsdp"), P()),
        check_vma=False,
    )
```

profile of v0, /device:TPU:0, one launch (start us, length us, event | category | flops | bytes accessed | tf_op | source)
XLA Modules:
  0.0 905.5 jit_solution(8188198296431997854)
XLA Ops:
  7.2 0.0 all-reduce.2.cloned.1.call-start
  7.2 24.2 %multiply_reduce_fusion = f32[4,6400]{1,0:T(4,128)S(1)} fusion(f32[4,6400,512]{2,1,0:T(8,128)} %param.4, bf16[4,6400,512]{2,1,0:T(8,128)(2,1)} %param.5), kind=kLoop, calls=%fused_computation.1 | loop fusion | flops 52403200 | bytes 78745600 | tf_op jit(solution)/shard_map/reduce_sum | solution.py:9
  31.4 2.3 copy.21
  33.7 0.0 all-reduce.2.cloned.1.call-update
  33.7 135.6 %all-reduce.2.cloned.1.call-done = f32[4,6400]{0,1:T(8,128)} async-done(((f32[4,6400]{0,1:T(8,128)}), f32[4,6400]{0,1:T(8,128)}) %all-reduce.2.cloned.1.call-update) | async-done | bytes 102416 | tf_op jit(solution)/shard_map/psum | solution.py:9
  169.3 2.7 sqrt.3
  172.0 1.2 copy.17
  173.3 34.3 %divide_convert_fusion = bf16[4,6400,512]{2,1,0:T(8,128)(2,1)} fusion(f32[4,6400,512]{2,1,0:T(8,128)} %param.4, bf16[4,6400,512]{2,1,0:T(8,128)(2,1)} %param.5, f32[4,6400]{1,0:T(4,128)S(1)} %copy.17), kind=kLoop, calls=%fused_computation | loop fusion | flops 52428800 | bytes 104960000 | tf_op jit(solution)/shard_map/convert_element_type | solution.py:11
  207.5 33.4 %copy.18 = bf16[4,6400,512]{2,0,1:T(4,128)(2,1)} copy(bf16[4,6400,512]{2,1,0:T(8,128)(2,1)} %divide_convert_fusion) | data formatting | bytes 52428800 | tf_op jit(solution)/shard_map/convert_element_type | solution.py:11
  240.9 0.0 copy-start
  240.9 0.0 copy-start.1
  240.9 6.6 all-to-all-start
  247.6 0.0 copy-done
  247.6 0.0 copy-done.1
  247.6 585.0 %all_gather.6 = bf16[4096,4]{0,1:T(4,128)(2,1)S(1)} all-gather(bf16[512,4]{0,1:T(4,128)(2,1)S(1)} %multiply_convert_fusion), channel_id=1, replica_groups=mesh['ep'=4,'fsdp'=8] {'fsdp'}, dimensions={0}, use_global_device_ids=true | all-gather | bytes 36864 | tf_op jit(solution)/shard_map/all_gather | solution.py:17
  832.7 5.4 all-gather
  838.1 0.7 reshape.9
  838.8 0.8 constant_dynamic-slice_fusion
  839.5 1.8 copy.20
  841.3 0.0 all-to-all-done
  841.3 18.2 %copy.19 = bf16[4,800,8,512]{3,2,1,0:T(8,128)(2,1)} copy(bf16[4,800,8,512]{3,0,1,2:T(4,128)(2,1)} %bitcast.1) | data formatting | bytes 52428800 | tf_op jit(solution)/shard_map/all_to_all | solution.py:12
  859.5 39.2 %all_to_all.16 = bf16[4,800,4096]{2,1,0:T(8,128)(2,1)} reshape(bf16[4,800,8,512]{3,2,1,0:T(8,128)(2,1)} %copy.19) | data formatting | bytes 52428800 | tf_op jit(solution)/shard_map/all_to_all | solution.py:12
  (1 shorter events, 0.0 us)
Async XLA Ops:
  7.2 162.2 %all-reduce.2.cloned.1.call-start = ((), (), s32[]{:S(2)}) async-start(), calls=%async_computation.1 | async-start | bytes 6553600 | tf_op jit(solution)/shard_map/psum | solution.py:9
  240.9 6.7 copy-start
  240.9 6.7 copy-start.1
  240.9 600.4 %all-to-all-start = ((bf16[4,6400,512]{2,0,1:T(4,128)(2,1)}), bf16[4,6400,512]{2,0,1:T(4,128)(2,1)}, u32[]{:S(2)}, u32[]{:S(2)}) async-start(bf16[4,6400,512]{2,0,1:T(4,128)(2,1)} %copy.18), calls=%async_computation | async-start | bytes 52428800 | tf_op jit(solution)/shard_map/all_to_all | solution.py:12
Sparse Core Ops, SparseCore 0:
  33.9 135.4 all-reduce.1
where the time goes:
time: 907 us; the launch traced here: 906 us
  blocking collectives  590 us (65%)
  waiting for transfers between devices  136 us (15%)
  local copies, waits for them, and re-layouts  100 us (11%)
  other arithmetic  58.5 us (6%)
  between operations  14.1 us (2%)
    all_gather x1, blocking collectives, shards(): row_router = lax.all_gather(part_router, 'fsdp', axis=0, tiled=True)  585 us
    psum x1, waiting for transfers between devices, shards(): total_down = lax.psum(jnp.sum(merged_down * merged_down, axis=2), 'fsdp')  136 us
    all_to_all x2, local copies, waits for them, and re-layouts, shards(): lax.all_to_all(narrow_down, 'fsdp', split_axis=1, concat_axis=2, tiled=True)  57.4 us
    convert_element_type x1, other arithmetic, shards(): (merged_down / jnp.expand_dims(scale_down, 2)).astype(jnp.bfloat16)  34.3 us
    convert_element_type x1, local copies, waits for them, and re-layouts, shards(): (merged_down / jnp.expand_dims(scale_down, 2)).astype(jnp.bfloat16)  33.4 us
    reduce_sum x1, other arithmetic, shards(): total_down = lax.psum(jnp.sum(merged_down * merged_down, axis=2), 'fsdp')  24.2 us
  transfers between devices with their start and end apart: 2, of which 1 were waited for; matrix products, arithmetic and copies ran while one was open for 0% of the time, Pallas kernels for 0%

commit v1 on v0

v1 whole, which is shorter than its diff:
```python
import jax
import jax.numpy as jnp
from jax import lax
from jax.experimental import pallas as pl
from jax.experimental.pallas import tpu as pltpu
from jax.sharding import PartitionSpec as P


def place(held, pieces, expert, experts):
    shards, rows, cols = pieces.shape

    def body(*refs):
        refs[-1][...] = refs[-2][...]

    piece_spec = pl.BlockSpec((None, rows, cols), lambda s: (s, 0, 0))
    return pl.pallas_call(
        body,
        grid=(shards,),
        in_specs=([] if held is None else [pl.BlockSpec(memory_space=pl.ANY)]) + [piece_spec],
        out_specs=pl.BlockSpec((None, rows, cols), lambda s: (expert, 0, s)),
        out_shape=jax.ShapeDtypeStruct((experts, rows, shards * cols), pieces.dtype),
        input_output_aliases={} if held is None else {0: 0},
        cost_estimate=pl.CostEstimate(flops=50 * pieces.size, transcendentals=0, bytes_accessed=4 * pieces.size),
        name="place",
    )(*([] if held is None else [held]), pieces)


def shards(master_down, second_down, router_weight, router_gain):
    experts, width, cols = master_down.shape
    count = lax.axis_size("fsdp")
    rows = width // count

    part_router = (router_weight * router_gain[:, None]).astype(jnp.bfloat16)
    all_router = lax.all_gather(part_router.T, ("ep", "fsdp"), axis=0, tiled=False)

    merged_down = master_down + second_down.astype(jnp.float32)
    part_total = jnp.sum(merged_down * merged_down, axis=2)
    total_down = jnp.sum(lax.all_gather(part_total, "fsdp", axis=0, tiled=False), axis=0)
    scale_down, all_router = lax.optimization_barrier((jnp.sqrt(total_down), all_router))

    scaled = []
    for expert in range(experts):
        if scaled:
            master_down, second_down, scaled[-1] = lax.optimization_barrier((master_down, second_down, scaled[-1]))
        merged = master_down[expert] + second_down[expert].astype(jnp.float32)
        scaled.append((merged / scale_down[expert][:, None]).astype(jnp.bfloat16))
    received = [lax.all_to_all(part, "fsdp", split_axis=0, concat_axis=0, tiled=True) for part in scaled]
    final_down = None
    for expert in range(experts):
        final_down = place(final_down, received[expert].reshape(count, rows, cols), expert, experts)

    groups = all_router.shape[0] // count
    serve_router = all_router.reshape(groups, count, *part_router.T.shape).transpose(1, 3, 0, 2)
    serve_router = serve_router.reshape(count * part_router.shape[0], groups * part_router.shape[1])
    own_scale = lax.dynamic_slice_in_dim(scale_down, lax.axis_index("fsdp") * rows, rows, axis=1)
    return (final_down, own_scale, serve_router)


def solution(mesh):
    return jax.shard_map(
        shards,
        mesh=mesh,
        in_specs=(P("ep", None, "fsdp"), P("ep", None, "fsdp"), P("fsdp", "ep"), P("fsdp")),
        out_specs=(P("ep", "fsdp", None), P("ep", "fsdp"), P()),
        check_vma=False,
    )
```

time: 907 us -> 733 us (0.81)
  blocking collectives: 590 us -> 99.4 us
  waiting for transfers between devices: 136 us -> 511 us
  local copies, waits for them, and re-layouts: 100 us -> 1.81 us
  Pallas kernels: 0 us -> 31.7 us
  between operations: 14.1 us -> 0.75 us
  starting transfers between devices: 6.67 us -> 19.1 us
  other arithmetic: 58.5 us -> 68.1 us
    all_to_all x1 -> x4, waiting for transfers between devices: 0.01 us -> 511 us  [shards(): lax.all_to_all(part, 'fsdp', split_axis=0, concat_axis=0, tiled=True)]
    all_gather x2, blocking collectives: 590 us -> 99.4 us  [the longest x1 65.5 us: shards(): lax.all_gather(part_router.T, ('ep', 'fsdp'), axis=0, tiled=False)]
    psum x1 -> x0, waiting for transfers between devices: 136 us -> none  [shards(): total_down = lax.psum(jnp.sum(merged_down * merged_down, axis=2), 'fsdp')]
    all_to_all x2 -> x0, local copies, waits for them, and re-layouts: 57.4 us -> none  [shards(): lax.all_to_all(narrow_down, 'fsdp', split_axis=1, concat_axis=2, tiled=True)]
    convert_element_type x1 -> x0, local copies, waits for them, and re-layouts: 33.4 us -> none  [shards(): (merged_down / jnp.expand_dims(scale_down, 2)).astype(jnp.bfloat16)]
    pallas_call x0 -> x4, Pallas kernels: none -> 31.7 us  [place(): pl.pallas_call(body, grid=(shards,), in_specs=([] if held is None else [p...]
    all_to_all x1 -> x4, starting transfers between devices: 6.63 us -> 19.1 us  [shards(): lax.all_to_all(part, 'fsdp', split_axis=0, concat_axis=0, tiled=True)]
    convert_element_type x2 -> x4, other arithmetic: 34.3 us -> 36.1 us  [shards(): scaled.append((merged / scale_down[expert][:, None]).astype(jnp.bfloat16))]
  transfers between devices with their start and end apart: 2 -> 4, of which waited for: 1 -> 4; matrix products, arithmetic and copies ran while one was open for 0% -> 5% of each run, Pallas kernels for 0% -> 3%
where the time goes in v1:
time: 733 us; the launch traced here: 732 us
  waiting for transfers between devices  511 us (70%)
  blocking collectives  99.4 us (14%)
  other arithmetic  68.1 us (9%)
  Pallas kernels  31.7 us (4%)
  starting transfers between devices  19.1 us (3%)
    all_to_all x4, waiting for transfers between devices, shards(): lax.all_to_all(part, 'fsdp', split_axis=0, concat_axis=0, tiled=True)  511 us
    all_gather x1, blocking collectives, shards(): lax.all_gather(part_router.T, ('ep', 'fsdp'), axis=0, tiled=False)  65.5 us
    convert_element_type x4, other arithmetic, shards(): scaled.append((merged / scale_down[expert][:, None]).astype(jnp.bfloat16))  36.1 us
    all_gather x1, blocking collectives, shards(): lax.all_gather(part_total, 'fsdp', axis=0, tiled=False)  33.9 us
    pallas_call x4, Pallas kernels, place(): pl.pallas_call(body, grid=(shards,), in_specs=([] if held is None else [p...  31.7 us
    reduce_sum x1, other arithmetic, shards(): part_total = jnp.sum(merged_down * merged_down, axis=2)  24.2 us
    all_to_all x4, starting transfers between devices, shards(): lax.all_to_all(part, 'fsdp', split_axis=0, concat_axis=0, tiled=True)  19.1 us
  transfers between devices with their start and end apart: 4, of which 4 were waited for; matrix products, arithmetic and copies ran while one was open for 5% of the time, Pallas kernels for 3%

profile of v1, /device:TPU:0, one launch (start us, length us, event | category | flops | bytes accessed | tf_op | source)
XLA Modules:
  0.0 731.8 jit_solution(1005521565383726174)
XLA Ops:
  0.6 0.0 copy-start
  0.6 0.0 copy-start.1
  0.7 24.2 %multiply_reduce_fusion = f32[4,6400]{1,0:T(4,128)S(1)} fusion(f32[4,6400,512]{2,1,0:T(8,128)} %param.4, bf16[4,6400,512]{2,1,0:T(8,128)(2,1)} %param.5), kind=kLoop, calls=%fused_computation | loop fusion | flops 52403200 | bytes 78745600 | tf_op jit(solution)/shard_map/reduce_sum | solution.py:37
  24.9 33.9 %all-gather.2 = f32[8,4,6400]{2,1,0:T(4,128)S(1)} all-gather(f32[1,4,6400]{2,1,0:T(4,128)S(1)} %bitcast.35), channel_id=2, replica_groups=mesh['ep'=4,'fsdp'=8] {'fsdp'}, dimensions={0}, use_global_device_ids=true | all-gather | bytes 921600 | tf_op jit(solution)/shard_map/all_gather | solution.py:38
  58.8 0.1 reduce_sum.19
  58.9 0.1 sqrt.3
  59.0 0.0 copy-done
  59.0 0.0 copy-done.1
  59.0 65.5 %all-gather.3 = bf16[32,4,512]{2,1,0:T(4,128)(2,1)S(1)} all-gather(bf16[1,4,512]{2,1,0:T(4,128)(2,1)S(1)} %fusion.3), channel_id=3, replica_groups=mesh['ep'=4,'fsdp'=8] {'ep','fsdp'}, dimensions={0}, use_global_device_ids=true | all-gather | bytes 135168 | tf_op jit(solution)/shard_map/all_gather | solution.py:34
  124.5 0.3 slice_reduce_fusion
  124.8 10.8 %fusion.2 = bf16[6400,512]{1,0:T(8,128)(2,1)} fusion(f32[4,6400,512]{2,1,0:T(8,128)} %param.4, f32[6400]{0:T(1024)S(1)} %get-tuple-element.28, bf16[4,6400,512]{2,1,0:T(8,128)(2,1)} %param.5), kind=kLoop, calls=%fused_computation.6 | loop fusion | flops 13107200 | bytes 26240000 | tf_op jit(solution)/shard_map/convert_element_type | solution.py:46
  135.6 4.8 all-to-all-start
  140.4 10.9 %fusion.1 = bf16[6400,512]{1,0:T(8,128)(2,1)} fusion(f32[4,6400,512]{2,1,0:T(8,128)} %param.4, f32[6400]{0:T(1024)S(1)} %get-tuple-element.27, bf16[4,6400,512]{2,1,0:T(8,128)(2,1)} %param.5), kind=kLoop, calls=%fused_computation.4 | loop fusion | flops 13107200 | bytes 26240000 | tf_op jit(solution)/shard_map/convert_element_type | solution.py:46
  151.3 129.6 %all-to-all-done.refs_0_ = bf16[8,800,512]{2,1,0:T(8,128)(2,1)} async-done(((bf16[8,800,512]{2,1,0:T(8,128)(2,1)}), bf16[8,800,512]{2,1,0:T(8,128)(2,1)}, u32[]{:S(2)}, u32[]{:S(2)}) %all-to-all-start) | async-done | bytes 6553632 | tf_op jit(solution)/shard_map/all_to_all | solution.py:47
  280.8 4.8 all-to-all-start.1
  285.6 10.8 %fusion = bf16[6400,512]{1,0:T(8,128)(2,1)} fusion(f32[4,6400,512]{2,1,0:T(8,128)} %param.4, f32[6400]{0:T(1024)S(1)} %get-tuple-element.26, bf16[4,6400,512]{2,1,0:T(8,128)(2,1)} %param.5), kind=kLoop, calls=%fused_computation.2 | loop fusion | flops 13107200 | bytes 26240000 | tf_op jit(solution)/shard_map/convert_element_type | solution.py:46
  296.5 132.0 %all-to-all-done.1.refs_1_ = bf16[8,800,512]{2,1,0:T(8,128)(2,1)} async-done(((bf16[8,800,512]{2,1,0:T(8,128)(2,1)}), bf16[8,800,512]{2,1,0:T(8,128)(2,1)}, u32[]{:S(2)}, u32[]{:S(2)}) %all-to-all-start.1) | async-done | bytes 6553632 | tf_op jit(solution)/shard_map/all_to_all | solution.py:47
  428.5 4.8 all-to-all-start.2
  433.3 0.1 div.50
  433.4 7.7 %convert_add_fusion = f32[1,6400,512]{2,1,0:T(8,128)S(1)} fusion(f32[4,6400,512]{2,1,0:T(8,128)} %param.4, bf16[4,6400,512]{2,1,0:T(8,128)(2,1)} %param.5), kind=kLoop, calls=%fused_computation.8 | loop fusion | flops 6553600 | bytes 32768000 | tf_op jit(solution)/shard_map/add | solution.py:45
  441.1 3.5 divide_convert_fusion
  444.6 131.5 %all-to-all-done.2.refs_1_ = bf16[8,800,512]{2,1,0:T(8,128)(2,1)} async-done(((bf16[8,800,512]{2,1,0:T(8,128)(2,1)}), bf16[8,800,512]{2,1,0:T(8,128)(2,1)}, u32[]{:S(2)}, u32[]{:S(2)}) %all-to-all-start.2) | async-done | bytes 6553632 | tf_op jit(solution)/shard_map/all_to_all | solution.py:47
  576.1 4.8 all-to-all-start.3
  580.9 0.7 copy.12
  581.6 0.7 constant_dynamic-slice_fusion
  582.3 7.9 %place.4.refs_0_ = bf16[4,800,4096]{2,1,0:T(8,128)(2,1)} custom-call(bf16[8,800,512]{2,1,0:T(8,128)(2,1)} %all-to-all-done.refs_0_), custom_call_target="tpu_custom_call" | custom-call | flops 163840000 | bytes 13107200 | tf_op jit(solution)/shard_map/place/pallas_call | solution.py:16
  590.2 7.9 %place.5.refs_0_ = bf16[4,800,4096]{2,1,0:T(8,128)(2,1)} custom-call(bf16[4,800,4096]{2,1,0:T(8,128)(2,1)} %place.4.refs_0_, bf16[8,800,512]{2,1,0:T(8,128)(2,1)} %all-to-all-done.1.refs_1_), custom_call_target="tpu_custom_call", output_to_operand_aliasing={{}: (0, {})} | custom-call | flops 163840000 | bytes 13107200 | tf_op jit(solution)/shard_map/place/pallas_call | solution.py:16
  598.1 7.9 %place.6.refs_0_ = bf16[4,800,4096]{2,1,0:T(8,128)(2,1)} custom-call(bf16[4,800,4096]{2,1,0:T(8,128)(2,1)} %place.5.refs_0_, bf16[8,800,512]{2,1,0:T(8,128)(2,1)} %all-to-all-done.2.refs_1_), custom_call_target="tpu_custom_call", output_to_operand_aliasing={{}: (0, {})} | custom-call | flops 163840000 | bytes 13107200 | tf_op jit(solution)/shard_map/place/pallas_call | solution.py:16
  606.1 117.8 %all-to-all-done.3.refs_1_ = bf16[8,800,512]{2,1,0:T(8,128)(2,1)} async-done(((bf16[8,800,512]{2,1,0:T(8,128)(2,1)}), bf16[8,800,512]{2,1,0:T(8,128)(2,1)}, u32[]{:S(2)}, u32[]{:S(2)}) %all-to-all-start.3) | async-done | bytes 6553632 | tf_op jit(solution)/shard_map/all_to_all | solution.py:47
  723.8 7.9 %place.7 = bf16[4,800,4096]{2,1,0:T(8,128)(2,1)} custom-call(bf16[4,800,4096]{2,1,0:T(8,128)(2,1)} %place.6.refs_0_, bf16[8,800,512]{2,1,0:T(8,128)(2,1)} %all-to-all-done.3.refs_1_), custom_call_target="tpu_custom_call", output_to_operand_aliasing={{}: (0, {})} | custom-call | flops 163840000 | bytes 13107200 | tf_op jit(solution)/shard_map/place/pallas_call | solution.py:16
  (2 shorter events, 0.0 us)
Async XLA Ops:
  0.6 58.4 %copy-start = (f32[512,4]{0,1:T(4,128)S(1)}, f32[512,4]{0,1:T(4,128)}, u32[]{:S(2)}) copy-start(f32[512,4]{0,1:T(4,128)} %param.6) | copy-start | bytes 24580
  0.6 58.4 %copy-start.1 = (f32[512]{0:T(512)S(1)}, f32[512]{0:T(512)}, u32[]{:S(2)}) copy-start(f32[512]{0:T(512)} %param.7) | copy-start | bytes 6148
  135.6 145.2 %all-to-all-start = ((bf16[8,800,512]{2,1,0:T(8,128)(2,1)}), bf16[8,800,512]{2,1,0:T(8,128)(2,1)}, u32[]{:S(2)}, u32[]{:S(2)}) async-start(bf16[8,800,512]{2,1,0:T(8,128)(2,1)} %bitcast.32), calls=%async_computation | async-start | bytes 13107200 | tf_op jit(solution)/shard_map/all_to_all | solution.py:47
  280.8 147.7 %all-to-all-start.1 = ((bf16[8,800,512]{2,1,0:T(8,128)(2,1)}), bf16[8,800,512]{2,1,0:T(8,128)(2,1)}, u32[]{:S(2)}, u32[]{:S(2)}) async-start(bf16[8,800,512]{2,1,0:T(8,128)(2,1)} %bitcast.31), calls=%async_computation.1 | async-start | bytes 13107200 | tf_op jit(solution)/shard_map/all_to_all | solution.py:47
  428.5 147.6 %all-to-all-start.2 = ((bf16[8,800,512]{2,1,0:T(8,128)(2,1)}), bf16[8,800,512]{2,1,0:T(8,128)(2,1)}, u32[]{:S(2)}, u32[]{:S(2)}) async-start(bf16[8,800,512]{2,1,0:T(8,128)(2,1)} %bitcast.30), calls=%async_computation.2 | async-start | bytes 13107200 | tf_op jit(solution)/shard_map/all_to_all | solution.py:47
  576.1 147.7 %all-to-all-start.3 = ((bf16[8,800,512]{2,1,0:T(8,128)(2,1)}), bf16[8,800,512]{2,1,0:T(8,128)(2,1)}, u32[]{:S(2)}, u32[]{:S(2)}) async-start(bf16[8,800,512]{2,1,0:T(8,128)(2,1)} %divide_convert_fusion), calls=%async_computation.3 | async-start | bytes 13107200 | tf_op jit(solution)/shard_map/all_to_all | solution.py:47

commit v2 on v1

v2 whole, which is shorter than its diff:
```python
import jax
import jax.numpy as jnp
from jax import lax
from jax.experimental import pallas as pl
from jax.experimental.pallas import tpu as pltpu
from jax.sharding import PartitionSpec as P


def place(held, pieces, expert, experts):
    shards, rows, cols = pieces.shape

    def body(*refs):
        refs[-1][...] = refs[-2][...]

    block = rows // 2 if rows % 32 == 0 else rows
    piece_spec = pl.BlockSpec((None, block, cols), lambda s, r: (s, r, 0))
    return pl.pallas_call(
        body,
        grid=(shards, rows // block),
        in_specs=([] if held is None else [pl.BlockSpec(memory_space=pl.ANY)]) + [piece_spec],
        out_specs=pl.BlockSpec((None, block, cols), lambda s, r: (expert, r, s)),
        out_shape=jax.ShapeDtypeStruct((experts, rows, shards * cols), pieces.dtype),
        input_output_aliases={} if held is None else {0: 0},
        cost_estimate=pl.CostEstimate(flops=50 * pieces.size, transcendentals=0, bytes_accessed=4 * pieces.size),
        name="place",
    )(*([] if held is None else [held]), pieces)


def shards(master_down, second_down, router_weight, router_gain):
    experts, width, cols = master_down.shape
    count = lax.axis_size("fsdp")
    rows = width // count

    merged_down = master_down + second_down.astype(jnp.float32)
    part_total = jnp.sum(merged_down * merged_down, axis=2).reshape(experts, count, rows).transpose(1, 0, 2)
    totals = lax.all_to_all(part_total, "fsdp", split_axis=0, concat_axis=0, tiled=True)
    own_scale = jnp.sqrt(jnp.sum(totals, axis=0))
    copies = jnp.broadcast_to(own_scale[None], (count, *own_scale.shape))
    scale_down = lax.all_to_all(copies, "fsdp", split_axis=0, concat_axis=0, tiled=True)

    part_router = (router_weight * router_gain[:, None]).astype(jnp.bfloat16).T
    scaled = []
    for expert in range(experts):
        if scaled:
            master_down, second_down, scaled[-1] = lax.optimization_barrier((master_down, second_down, scaled[-1]))
        merged = master_down[expert] + second_down[expert].astype(jnp.float32)
        scaled.append((merged / scale_down[:, expert].reshape(width, 1)).astype(jnp.bfloat16))
        if expert == 1:
            part_router, scaled[1] = lax.optimization_barrier((part_router, scaled[1]))
            part_router = lax.all_gather(part_router, "ep", axis=0, tiled=True)
    part_router, scaled[-1] = lax.optimization_barrier((part_router, scaled[-1]))
    serve_router = lax.all_gather(part_router, "fsdp", axis=1, tiled=True)
    serve_router, scaled[-1] = lax.optimization_barrier((serve_router, scaled[-1]))
    serve_router = serve_router.T
    received = [lax.all_to_all(part, "fsdp", split_axis=0, concat_axis=0, tiled=True) for part in scaled]
    final_down = None
    for expert in range(experts):
        final_down = place(final_down, received[expert].reshape(count, rows, cols), expert, experts)
    return (final_down, own_scale, serve_router)


def solution(mesh):
    return jax.shard_map(
        shards,
        mesh=mesh,
        in_specs=(P("ep", None, "fsdp"), P("ep", None, "fsdp"), P("fsdp", "ep"), P("fsdp")),
        out_specs=(P("ep", "fsdp", None), P("ep", "fsdp"), P()),
        check_vma=False,
    )
```

time: 733 us -> 679 us (0.926)
  waiting for transfers between devices: 511 us -> 368 us
  blocking collectives: 99.4 us -> 176 us
  Pallas kernels: 31.7 us -> 44.2 us
    all_to_all x4, waiting for transfers between devices: 511 us -> 368 us  [shards(): lax.all_to_all(part, 'fsdp', split_axis=0, concat_axis=0, tiled=True)]
    all_gather x2, blocking collectives: 99.4 us -> 152 us  [the longest x1 147 us: shards(): serve_router = lax.all_gather(part_router, 'fsdp', axis=1, tiled=True)]
    all_to_all x0 -> x2, blocking collectives: none -> 23.9 us  [the longest x1 14.3 us: shards(): lax.all_to_all(part_total, 'fsdp', split_axis=0, concat_axis=0, tiled=True)]
    pallas_call x4, Pallas kernels: 31.7 us -> 44.2 us  [place(): pl.pallas_call(body, grid=(shards, rows // block), in_specs=([] if held i...]
    add x1 -> x0, other arithmetic: 7.68 us -> none  [shards(): merged = master_down[expert] + second_down[expert].astype(jnp.float32)]
    convert_element_type x4, other arithmetic: 36.1 us -> 43.4 us  [shards(): (merged / scale_down[:, expert].reshape(width, 1)).astype(jnp.bfloat16)]
  transfers between devices with their start and end apart: 4 -> 4, of which waited for: 4 -> 3; matrix products, arithmetic and copies ran while one was open for 5% -> 5% of each run, Pallas kernels for 3% -> 5%
where the time goes in v2:
time: 679 us; the launch traced here: 677 us
  waiting for transfers between devices  368 us (54%)
  blocking collectives  176 us (26%)
  other arithmetic  67.7 us (10%)
  Pallas kernels  44.2 us (7%)
  starting transfers between devices  19.3 us (3%)
    all_to_all x4, waiting for transfers between devices, shards(): lax.all_to_all(part, 'fsdp', split_axis=0, concat_axis=0, tiled=True)  368 us
    all_gather x1, blocking collectives, shards(): serve_router = lax.all_gather(part_router, 'fsdp', axis=1, tiled=True)  147 us
    pallas_call x4, Pallas kernels, place(): pl.pallas_call(body, grid=(shards, rows // block), in_specs=([] if held i...  44.2 us
    convert_element_type x4, other arithmetic, shards(): (merged / scale_down[:, expert].reshape(width, 1)).astype(jnp.bfloat16)  43.4 us
    reduce_sum x1, other arithmetic, shards(): jnp.sum(merged_down * merged_down, axis=2).reshape(experts, count, rows)  24.2 us
    all_to_all x4, starting transfers between devices, shards(): lax.all_to_all(part, 'fsdp', split_axis=0, concat_axis=0, tiled=True)  19.3 us
    all_to_all x1, blocking collectives, shards(): lax.all_to_all(part_total, 'fsdp', split_axis=0, concat_axis=0, tiled=True)  14.3 us
  transfers between devices with their start and end apart: 4, of which 3 were waited for; matrix products, arithmetic and copies ran while one was open for 5% of the time, Pallas kernels for 5%

profile of v2, /device:TPU:0, one launch (start us, length us, event | category | flops | bytes accessed | tf_op | source)
XLA Modules:
  0.0 677.1 jit_solution(7844088052583639073)
XLA Ops:
  0.6 24.2 %multiply_reduce_fusion = f32[4,6400]{1,0:T(4,128)S(1)} fusion(f32[4,6400,512]{2,1,0:T(8,128)} %param.4, bf16[4,6400,512]{2,1,0:T(8,128)(2,1)} %param.5), kind=kLoop, calls=%fused_computation | loop fusion | flops 52403200 | bytes 78745600 | tf_op jit(solution)/shard_map/reduce_sum | solution.py:35
  24.9 0.1 reshape.41
  25.0 14.3 %all_to_all.46 = f32[8,4,800]{2,1,0:T(4,128)S(1)} all-to-all(f32[8,4,800]{2,1,0:T(4,128)S(1)} %copy.10), channel_id=1, replica_groups=mesh['ep'=4,'fsdp'=8] {'fsdp'}, dimensions={0} | all-to-all | bytes 204800 | tf_op jit(solution)/shard_map/all_to_all | solution.py:36
  39.4 0.0 copy-start
  39.4 9.6 %all_to_all.47 = f32[8,4,800]{2,1,0:T(4,128)S(1)} all-to-all(f32[8,4,800]{2,1,0:T(4,128)S(1)} %broadcast_in_dim.2), channel_id=1, replica_groups=mesh['ep'=4,'fsdp'=8] {'fsdp'}, dimensions={0} | all-to-all | bytes 204800 | tf_op jit(solution)/shard_map/all_to_all | solution.py:39
  49.1 0.3 slice_reduce_fusion
  49.4 0.1 div.40
  49.4 10.8 %fusion.3 = bf16[6400,512]{1,0:T(8,128)(2,1)} fusion(f32[4,6400,512]{2,1,0:T(8,128)} %param.4, f32[6400]{0:T(1024)S(1)} %div.40, bf16[4,6400,512]{2,1,0:T(8,128)(2,1)} %param.5), kind=kLoop, calls=%fused_computation.8 | loop fusion | flops 13107200 | bytes 26240000 | tf_op jit(solution)/shard_map/convert_element_type | solution.py:47
  60.3 0.0 copy-done
  60.3 4.9 all-to-all-start.2
  65.2 0.0 copy-done.1
  65.2 0.0 copy-done.2
  65.3 0.1 div.43
  65.3 10.9 %fusion.2 = bf16[6400,512]{1,0:T(8,128)(2,1)} fusion(f32[4,6400,512]{2,1,0:T(8,128)} %param.4, f32[6400]{0:T(1024)S(1)} %div.43, bf16[4,6400,512]{2,1,0:T(8,128)(2,1)} %param.5), kind=kLoop, calls=%fused_computation.6 | loop fusion | flops 13107200 | bytes 26240000 | tf_op jit(solution)/shard_map/convert_element_type | solution.py:47
  76.2 130.6 %all-to-all-done.2.refs_0_ = bf16[8,800,512]{2,1,0:T(8,128)(2,1)} async-done(((bf16[8,800,512]{2,1,0:T(8,128)(2,1)}), bf16[8,800,512]{2,1,0:T(8,128)(2,1)}, u32[]{:S(2)}, u32[]{:S(2)}) %all-to-all-start.2) | async-done | bytes 6553632 | tf_op jit(solution)/shard_map/all_to_all | solution.py:55
  206.8 4.8 all-to-all-start.3
  211.6 0.1 div.46
  211.7 10.8 %fusion.1 = bf16[6400,512]{1,0:T(8,128)(2,1)} fusion(f32[4,6400,512]{2,1,0:T(8,128)} %param.4, f32[6400]{0:T(1024)S(1)} %div.46, bf16[4,6400,512]{2,1,0:T(8,128)(2,1)} %param.5), kind=kLoop, calls=%fused_computation.4 | loop fusion | flops 13107200 | bytes 26240000 | tf_op jit(solution)/shard_map/convert_element_type | solution.py:47
  222.5 131.9 %all-to-all-done.3.refs_1_ = bf16[8,800,512]{2,1,0:T(8,128)(2,1)} async-done(((bf16[8,800,512]{2,1,0:T(8,128)(2,1)}), bf16[8,800,512]{2,1,0:T(8,128)(2,1)}, u32[]{:S(2)}, u32[]{:S(2)}) %all-to-all-start.3) | async-done | bytes 6553632 | tf_op jit(solution)/shard_map/all_to_all | solution.py:55
  354.4 4.8 all-to-all-start.4
  359.2 5.2 all-gather
  364.5 0.1 div.49
  364.5 10.8 %fusion = bf16[6400,512]{1,0:T(8,128)(2,1)} fusion(f32[4,6400,512]{2,1,0:T(8,128)} %param.4, f32[6400]{0:T(1024)S(1)} %div.49, bf16[4,6400,512]{2,1,0:T(8,128)(2,1)} %param.5), kind=kLoop, calls=%fused_computation.2 | loop fusion | flops 13107200 | bytes 26240000 | tf_op jit(solution)/shard_map/convert_element_type | solution.py:47
  375.4 146.8 %all_gather.7 = bf16[16,4096]{1,0:T(8,128)(2,1)S(1)} all-gather(bf16[16,512]{1,0:T(8,128)(2,1)S(1)} %reshape.43), channel_id=1, replica_groups=mesh['ep'=4,'fsdp'=8] {'fsdp'}, dimensions={1}, use_global_device_ids=true | all-gather | bytes 147456 | tf_op jit(solution)/shard_map/all_gather | solution.py:52
  522.2 0.0 all-to-all-done.4.refs_1_
  522.2 4.8 all-to-all-start.5
  527.0 11.1 %place.4.refs_0_ = bf16[4,800,4096]{2,1,0:T(8,128)(2,1)} custom-call(bf16[8,800,512]{2,1,0:T(8,128)(2,1)} %all-to-all-done.2.refs_0_), custom_call_target="tpu_custom_call" | custom-call | flops 163840000 | bytes 13107200 | tf_op jit(solution)/shard_map/place/pallas_call | solution.py:17
  538.0 11.0 %place.5.refs_0_ = bf16[4,800,4096]{2,1,0:T(8,128)(2,1)} custom-call(bf16[4,800,4096]{2,1,0:T(8,128)(2,1)} %place.4.refs_0_, bf16[8,800,512]{2,1,0:T(8,128)(2,1)} %all-to-all-done.3.refs_1_), custom_call_target="tpu_custom_call", output_to_operand_aliasing={{}: (0, {})} | custom-call | flops 163840000 | bytes 13107200 | tf_op jit(solution)/shard_map/place/pallas_call | solution.py:17
  549.1 11.0 %place.6.refs_0_ = bf16[4,800,4096]{2,1,0:T(8,128)(2,1)} custom-call(bf16[4,800,4096]{2,1,0:T(8,128)(2,1)} %place.5.refs_0_, bf16[8,800,512]{2,1,0:T(8,128)(2,1)} %all-to-all-done.4.refs_1_), custom_call_target="tpu_custom_call", output_to_operand_aliasing={{}: (0, {})} | custom-call | flops 163840000 | bytes 13107200 | tf_op jit(solution)/shard_map/place/pallas_call | solution.py:17
  560.1 105.3 %all-to-all-done.5.refs_1_ = bf16[8,800,512]{2,1,0:T(8,128)(2,1)} async-done(((bf16[8,800,512]{2,1,0:T(8,128)(2,1)}), bf16[8,800,512]{2,1,0:T(8,128)(2,1)}, u32[]{:S(2)}, u32[]{:S(2)}) %all-to-all-start.5) | async-done | bytes 6553632 | tf_op jit(solution)/shard_map/all_to_all | solution.py:55
  665.4 11.0 %place.7 = bf16[4,800,4096]{2,1,0:T(8,128)(2,1)} custom-call(bf16[4,800,4096]{2,1,0:T(8,128)(2,1)} %place.6.refs_0_, bf16[8,800,512]{2,1,0:T(8,128)(2,1)} %all-to-all-done.5.refs_1_), custom_call_target="tpu_custom_call", output_to_operand_aliasing={{}: (0, {})} | custom-call | flops 163840000 | bytes 13107200 | tf_op jit(solution)/shard_map/place/pallas_call | solution.py:17
  676.4 0.7 copy.15
  (8 shorter events, 0.1 us)
Async XLA Ops:
  39.4 20.9 %copy-start = (f32[4,800]{1,0:T(4,128)}, f32[4,800]{1,0:T(4,128)S(1)}, u32[]{:S(2)}) copy-start(f32[4,800]{1,0:T(4,128)S(1)} %sqrt.7) | copy-start | bytes 38404
  60.3 4.9 copy-start.1
  60.3 4.9 copy-start.2
  60.3 146.5 %all-to-all-start.2 = ((bf16[8,800,512]{2,1,0:T(8,128)(2,1)}), bf16[8,800,512]{2,1,0:T(8,128)(2,1)}, u32[]{:S(2)}, u32[]{:S(2)}) async-start(bf16[8,800,512]{2,1,0:T(8,128)(2,1)} %bitcast.28), calls=%async_computation.2 | async-start | bytes 13107200 | tf_op jit(solution)/shard_map/all_to_all | solution.py:55
  206.8 147.6 %all-to-all-start.3 = ((bf16[8,800,512]{2,1,0:T(8,128)(2,1)}), bf16[8,800,512]{2,1,0:T(8,128)(2,1)}, u32[]{:S(2)}, u32[]{:S(2)}) async-start(bf16[8,800,512]{2,1,0:T(8,128)(2,1)} %bitcast.27), calls=%async_computation.3 | async-start | bytes 13107200 | tf_op jit(solution)/shard_map/all_to_all | solution.py:55
  354.4 167.8 %all-to-all-start.4 = ((bf16[8,800,512]{2,1,0:T(8,128)(2,1)}), bf16[8,800,512]{2,1,0:T(8,128)(2,1)}, u32[]{:S(2)}, u32[]{:S(2)}) async-start(bf16[8,800,512]{2,1,0:T(8,128)(2,1)} %bitcast.25), calls=%async_computation.4 | async-start | bytes 13107200 | tf_op jit(solution)/shard_map/all_to_all | solution.py:55
  522.2 143.2 %all-to-all-start.5 = ((bf16[8,800,512]{2,1,0:T(8,128)(2,1)}), bf16[8,800,512]{2,1,0:T(8,128)(2,1)}, u32[]{:S(2)}, u32[]{:S(2)}) async-start(bf16[8,800,512]{2,1,0:T(8,128)(2,1)} %bitcast.26), calls=%async_computation.5 | async-start | bytes 13107200 | tf_op jit(solution)/shard_map/all_to_all | solution.py:55
